TPU v7x, 32 devices: a whole 2x2x4 slice. The times are simulated.
32 devices in a mesh: hst: 4 (over y, core), dev: 8 (over z, x).
Axes of the slice: x: 2, y: 2, z: 4, core: 2. Of those that a mesh axis runs over, the one named last changes fastest.
Arguments:
- hot_rows: bfloat16 [4096, 768], replicated, may hold values from -6 to 6
- cold_rows: bfloat16 [32768, 768], P(('hst', 'dev')), may hold values from -6 to 6
- hot_mask: int32 [65536], P(('hst', 'dev')), may hold values from 0 to 1, as said below
- hot_id: int32 [65536], P(('hst', 'dev')), may hold values from 0 to 4095
- cold_owner: int32 [65536], P(('hst', 'dev')), may hold values from 0 to 31, as said below
- cold_pos: int32 [65536], P(('hst', 'dev')), may hold values from 0 to 63, as said below
- cold_send: int32 [32, 2048], P(('hst', 'dev')), may hold values from 0 to 1023
- adjacency_one: int32 [65536, 15], P(('hst', 'dev')), may hold values from 0 to 2047
- adjacency_two: int32 [16384, 15], P(('hst', 'dev')), may hold values from 0 to 2303
- halo_send: int32 [32, 256], P(('hst', 'dev')), may hold values from 0 to 2047
- self_first: bfloat16 [768, 1024], replicated, may hold values from -0.21875 to 0.21875
- neigh_first: bfloat16 [768, 1024], replicated, may hold values from -0.21875 to 0.21875
- bn_gain: float32 [1024], replicated, may hold values from 0.1 to 1.9
- bn_shift: float32 [1024], replicated, may hold values from -3 to 3
- self_second: bfloat16 [1024, 153], replicated, may hold values from -0.1875 to 0.1875
- neigh_second: bfloat16 [1024, 153], replicated, may hold values from -0.1875 to 0.1875
Outputs:
- logits: float32 [16384, 153], P(('hst', 'dev'))
Inputs may be any that keep to these rules, and one draw needn't show every extreme that they name: Each device has exactly 1536 nodes with hot_mask 0. `cold_owner`: for each device and owner, at most 64 of the device's nodes with hot_mask 0 name that owner; some owner is named by exactly 64 of them on every device. `cold_pos`: the nodes of one device with hot_mask 0 and the same owner have distinct slots.
All inputs are finite; a program needn't handle non-finite values.
Results may differ from a plain program's by a relative error of at most 0.003.
The roundings to bfloat16 on the way count: a program that leaves them out, or rounds other values in their place, can miss the bound.
Values may be sent and summed in bfloat16 or wider, within the bound.
A program may use at most 128 MiB of HBM per device.

v0:
```python
import jax
import jax.numpy as jnp
from jax import lax
from jax.sharding import PartitionSpec as P

epsilon = 1e-05


def neighbour_mean(table, neighbours, fanout):
    columns = jnp.arange(table.shape[0], dtype=jnp.int32)
    counts = jnp.zeros((neighbours.shape[0], table.shape[0]), jnp.int32)
    for column in range(fanout):
        counts = counts + (neighbours[:, column : column + 1] == columns[None, :]).astype(jnp.int32)
    total = jnp.dot(counts.astype(jnp.bfloat16), table, preferred_element_type=jnp.float32)
    return (total / fanout).astype(jnp.bfloat16)


def local(
    hot_rows,
    cold_rows,
    hot_mask,
    hot_id,
    cold_owner,
    cold_pos,
    cold_send,
    adjacency_one,
    adjacency_two,
    halo_send,
    self_first,
    neigh_first,
    bn_gain,
    bn_shift,
    self_second,
    neigh_second,
):
    hosts = lax.axis_size("hst")
    within = lax.axis_size("dev")
    outgoing = jnp.take(cold_rows, cold_send[0], axis=0)
    slots = outgoing.shape[0] // (hosts * within)
    arrived = lax.all_to_all(outgoing, ("hst", "dev"), split_axis=0, concat_axis=0, tiled=True)
    cold_feat = jnp.take(arrived, cold_owner * slots + cold_pos, axis=0)
    hot_feat = jnp.take(hot_rows, hot_id, axis=0)
    features = jnp.where(hot_mask[:, None] == 1, hot_feat, cold_feat)
    first_mean = neighbour_mean(features, adjacency_one, adjacency_one.shape[1])
    hidden_pre = jnp.dot(features, self_first, preferred_element_type=jnp.float32) + jnp.dot(
        first_mean, neigh_first, preferred_element_type=jnp.float32
    )
    total_rows = hidden_pre.shape[0] * hosts * within
    sums, squares = lax.psum(
        (jnp.sum(hidden_pre, axis=0), jnp.sum(hidden_pre * hidden_pre, axis=0)), ("hst", "dev")
    )
    mean = sums / total_rows
    variance = squares / total_rows - mean * mean
    hidden = jax.nn.relu(
        (hidden_pre - mean) * lax.rsqrt(variance + epsilon) * bn_gain + bn_shift
    ).astype(jnp.bfloat16)
    boundary = jnp.take(hidden, halo_send[0], axis=0)
    received = lax.all_to_all(boundary, "dev", split_axis=0, concat_axis=0, tiled=True)
    table = jnp.concatenate([hidden, received], axis=0)
    targets = adjacency_two.shape[0]
    second_mean = neighbour_mean(table, adjacency_two, adjacency_two.shape[1])
    return jnp.dot(hidden[:targets], self_second, preferred_element_type=jnp.float32) + jnp.dot(
        second_mean, neigh_second, preferred_element_type=jnp.float32
    )


def solution(mesh):
    placed = (
        P(),
        P(("hst", "dev"), None),
        P(("hst", "dev")),
        P(("hst", "dev")),
        P(("hst", "dev")),
        P(("hst", "dev")),
        P(("hst", "dev"), None),
        P(("hst", "dev"), None),
        P(("hst", "dev"), None),
        P(("hst", "dev"), None),
        P(),
        P(),
        P(),
        P(),
        P(),
        P(),
    )
    return jax.shard_map(
        local, mesh=mesh, in_specs=placed, out_specs=P(("hst", "dev"), None), check_vma=False
    )
```

profile of v0, /device:TPU:8, one launch (start us, length us, event | category | flops | bytes accessed | tf_op | source)
XLA Modules:
  0.0 249.2 jit_solution(8531077166130631391)
XLA Ops:
  0.0 0.8 compare_select_fusion
  0.8 0.5 broadcast.108
  1.3 1.4 reduce.6
  2.7 0.1 squeeze.10
  2.8 11.7 %gather_fusion.1 = bf16[2048,768]{1,0:T(8,128)(2,1)} fusion(bf16[1024,768]{1,0:T(8,128)(2,1)} %param.17, s32[2048]{0:T(1024)S(1)} %broadcast_clamp_fusion.1), kind=kCustom, calls=%fused_computation.1 | custom fusion | bytes 6299648 | tf_op jit(solution)/shard_map/jit(_take)/gather | solution.py:38
  14.5 3.3 %broadcast_select_fusion = bf16[32,64,768]{2,1,0:T(8,128)(2,1)} fusion(bf16[32,64,768]{2,1,0:T(8,128)(2,1)} %bitcast.44, pred[32,64]{1,0:T(8,128)(4,1)S(1)} %compare_and_fusion), kind=kLoop, calls=%fused_computation.62 | loop fusion | flops 1572864 | bytes 6293504 | tf_op jit(solution)/shard_map/jit(_take)/select_n | solution.py:38
  17.8 6.1 %all-to-all-start = ((bf16[32,64,768]{2,1,0:T(8,128)(2,1)}), bf16[32,64,768]{2,1,0:T(8,128)(2,1)}, u32[]{:S(2)}, u32[]{:S(2)}) async-start(bf16[32,64,768]{2,1,0:T(8,128)(2,1)} %broadcast_select_fusion), calls=%async_computation | async-start | bytes 6291456 | tf_op jit(solution)/shard_map/all_to_all | solution.py:40
  23.9 0.7 reduce.7
  24.6 0.1 squeeze.12
  24.7 0.0 copy-start.7
  24.7 13.7 %gather_fusion = bf16[2048,768]{1,0:T(8,128)(2,1)} fusion(bf16[4096,768]{1,0:T(8,128)(2,1)} %param.16, s32[2048]{0:T(1024)S(1)} %fusion.43), kind=kCustom, calls=%fused_computation | custom fusion | bytes 6299648 | tf_op jit(solution)/shard_map/jit(_take)/gather | solution.py:42
  38.6 0.1 fusion.50
  38.7 53.6 %all-to-all-done = bf16[32,64,768]{2,1,0:T(8,128)(2,1)} async-done(((bf16[32,64,768]{2,1,0:T(8,128)(2,1)}), bf16[32,64,768]{2,1,0:T(8,128)(2,1)}, u32[]{:S(2)}, u32[]{:S(2)}) %all-to-all-start) | async-done | bytes 3145760 | tf_op jit(solution)/shard_map/all_to_all | solution.py:40
  92.3 12.3 %gather_fusion.2 = bf16[2048,768]{1,0:T(8,128)(2,1)} fusion(bf16[2048,768]{1,0:T(8,128)(2,1)} %bitcast.3, s32[2048]{0:T(1024)S(1)} %broadcast_clamp_fusion), kind=kCustom, calls=%fused_computation.2 | custom fusion | bytes 6299648 | tf_op jit(solution)/shard_map/jit(_take)/gather | solution.py:41
  104.6 8.4 %fusion.48 = f32[2048,1024]{1,0:T(8,128)} fusion(bf16[768,1024]{1,0:T(8,128)(2,1)} %param.26, bf16[2048,768]{1,0:T(8,128)(2,1)} %gather_fusion.2, bf16[2048,768]{1,0:T(8,128)(2,1)} %gather_fusion, pred[2048]{0:T(1024)(128)(4,1)S(1)} %get-tuple-element.42, pred[2048]{0:T(1024)(128)(4,1)S(1)} %get-tuple-element.43, pred[2048]{0:T(1024)(128)(4,1)S(1)} %broadcast_compare_fusion), kind=kOutput, calls=%fused_computation.104 | convolution fusion | flops 3225944064 | bytes 16259072 | tf_op jit(solution)/shard_map/dot_general | solution.py:45
  113.0 49.0 %fusion.49 = (f32[1024]{0:T(1024)S(1)}, f32[1024]{0:T(1024)S(1)}, f32[2048,1024]{1,0:T(8,128)}) fusion(f32[2048,1024]{1,0:T(8,128)} %fusion.48, bf16[768,1024]{1,0:T(8,128)(2,1)S(1)} %copy-done, s32[2048]{0:T(1024)S(1)} %bitcast.61, s32[2048]{0:T(1024)S(1)} %bitcast.62, s32[2048]{0:T(1024)S(1)} %bitcast.49, s32[2048]{0:T(1024)S(1)} %bitcast.50, ...), kind=kOutput, calls=%fused_computation.105 | convolution fusion | flops 9868670976 | bytes 24778752 | tf_op jit(solution)/shard_map/dot_general | solution.py:45
  162.0 42.2 %all-reduce = (f32[1024]{0:T(1024)S(1)}, f32[1024]{0:T(1024)S(1)}) all-reduce(f32[1024]{0:T(1024)S(1)} %get-tuple-element.6, f32[1024]{0:T(1024)S(1)} %get-tuple-element.5), channel_id=1, replica_groups=mesh['hst'=4,'dev'=8] {'hst','dev'}, use_global_device_ids=true, to_apply=%region_3.4 | all-reduce | flops 2048 | bytes 16384 | tf_op jit(solution)/shard_map/psum | solution.py:49
  204.2 6.9 %maximum_convert_fusion = bf16[2048,1024]{1,0:T(8,128)(2,1)} fusion(f32[2048,1024]{1,0:T(8,128)} %get-tuple-element.41, f32[1024]{0:T(1024)S(1)} %copy-done.8, f32[1024]{0:T(1024)S(1)} %copy-done.9, f32[1024]{0:T(1024)S(1)} %get-tuple-element.40, f32[1024]{0:T(1024)S(1)} %get-tuple-element.39), kind=kLoop, calls=%fused_computation.21 | loop fusion | flops 12582912 | bytes 12599296 | tf_op jit(solution)/shard_map/convert_element_type | solution.py:56
  211.1 4.3 %gather_fusion.3 = bf16[256,1024]{1,0:T(8,128)(2,1)S(1)} fusion(bf16[2048,1024]{1,0:T(8,128)(2,1)} %maximum_convert_fusion, s32[1024]{0:T(1024)S(1)} %pad_clamp_fusion), kind=kCustom, calls=%fused_computation.3 | custom fusion | bytes 1049600 | tf_op jit(solution)/shard_map/jit(_take)/gather | solution.py:57
  215.5 0.9 broadcast_select_fusion.1
  216.4 5.1 %all-to-all-start.1 = ((bf16[8,32,1024]{2,1,0:T(8,128)(2,1)}), bf16[8,32,1024]{2,1,0:T(8,128)(2,1)S(1)}, u32[]{:S(2)}, u32[]{:S(2)}) async-start(bf16[8,32,1024]{2,1,0:T(8,128)(2,1)} %broadcast_select_fusion.1), calls=%async_computation.1 | async-start | bytes 1048576 | tf_op jit(solution)/shard_map/all_to_all | solution.py:58
  221.5 12.3 %all-to-all-done.1 = bf16[8,32,1024]{2,1,0:T(8,128)(2,1)S(1)} async-done(((bf16[8,32,1024]{2,1,0:T(8,128)(2,1)}), bf16[8,32,1024]{2,1,0:T(8,128)(2,1)S(1)}, u32[]{:S(2)}, u32[]{:S(2)}) %all-to-all-start.1) | async-done | bytes 524320 | tf_op jit(solution)/shard_map/all_to_all | solution.py:58
  233.8 13.0 %fusion.39 = f32[512,153]{0,1:T(8,128)S(1)} fusion(bf16[1024,153]{0,1:T(8,128)(2,1)S(1)} %copy-done.11, bf16[256,1024]{1,0:T(8,128)(2,1)S(1)} %bitcast.46, bf16[2048,1024]{1,0:T(8,128)(2,1)} %maximum_convert_fusion, s32[512]{0:T(512)S(1)} %bitcast.77, s32[512]{0:T(512)S(1)} %bitcast.78, s32[512]{0:T(512)S(1)} %bitcast.65, s32[512]{0:T(512)S(1)} %bitcast.66, ...), kind=kOutput, calls=%fused_computation.79 | convolution fusion | flops 2639921152 | bytes 5376000 | tf_op jit(solution)/shard_map/dot_general | solution.py:62
  246.8 2.5 convolution_add_fusion.1
  (34 shorter events, 0.1 us)
Async XLA Ops:
  0.0 113.0 %copy-start = (bf16[768,1024]{1,0:T(8,128)(2,1)S(1)}, bf16[768,1024]{1,0:T(8,128)(2,1)}, u32[]{:S(2)}) copy-start(bf16[768,1024]{1,0:T(8,128)(2,1)} %param.27) | copy-start | bytes 4718596
  17.8 6.1 %copy-start.10 = (s32[1,256]{1,0:T(1,128)S(1)}, s32[1,256]{1,0:T(1,128)}, u32[]{:S(2)}) copy-start(s32[1,256]{1,0:T(1,128)} %param.25) | copy-start | bytes 3076
  17.8 6.9 %copy-start.5 = (s32[2048]{0:T(1024)S(1)}, s32[2048]{0:T(1024)}, u32[]{:S(2)}) copy-start(s32[2048]{0:T(1024)} %param.19) | copy-start | bytes 24580
  17.8 74.4 %all-to-all-start = ((bf16[32,64,768]{2,1,0:T(8,128)(2,1)}), bf16[32,64,768]{2,1,0:T(8,128)(2,1)}, u32[]{:S(2)}, u32[]{:S(2)}) async-start(bf16[32,64,768]{2,1,0:T(8,128)(2,1)} %broadcast_select_fusion), calls=%async_computation | async-start | bytes 6291456 | tf_op jit(solution)/shard_map/all_to_all | solution.py:40
  24.7 13.8 %copy-start.7 = (s32[2048]{0:T(1024)S(1)}, s32[2048]{0:T(1024)}, u32[]{:S(2)}) copy-start(s32[2048]{0:T(1024)} %param.18) | copy-start | bytes 24580
  24.7 13.8 %copy-start.3 = (s32[2048]{0:T(1024)S(1)}, s32[2048]{0:T(1024)}, u32[]{:S(2)}) copy-start(s32[2048]{0:T(1024)} %param.21) | copy-start | bytes 24580
  24.7 13.8 %copy-start.4 = (s32[2048]{0:T(1024)S(1)}, s32[2048]{0:T(1024)}, u32[]{:S(2)}) copy-start(s32[2048]{0:T(1024)} %param.20) | copy-start | bytes 24580
  24.7 13.9 %copy-start.2 = (s32[2048,15]{0,1:T(8,128)S(1)}, s32[2048,15]{0,1:T(8,128)}, u32[]{:S(2)}) copy-start(s32[2048,15]{0,1:T(8,128)} %param.23) | copy-start | bytes 368644
  113.0 91.2 %copy-start.8 = (f32[1024]{0:T(1024)S(1)}, f32[1024]{0:T(1024)}, u32[]{:S(2)}) copy-start(f32[1024]{0:T(1024)} %param.29) | copy-start | bytes 12292
  113.0 91.2 %copy-start.9 = (f32[1024]{0:T(1024)S(1)}, f32[1024]{0:T(1024)}, u32[]{:S(2)}) copy-start(f32[1024]{0:T(1024)} %param.28) | copy-start | bytes 12292
  211.1 10.3 %copy-start.6 = (s32[512,15]{0,1:T(8,128)S(1)}, s32[512,15]{0,1:T(8,128)}, u32[]{:S(2)}) copy-start(s32[512,15]{0,1:T(8,128)} %param.24) | copy-start | bytes 92164
  211.1 22.7 %copy-start.11 = (bf16[1024,153]{0,1:T(8,128)(2,1)S(1)}, bf16[1024,153]{0,1:T(8,128)(2,1)}, u32[]{:S(2)}) copy-start(bf16[1024,153]{0,1:T(8,128)(2,1)} %param.31) | copy-start | bytes 940036
  216.4 17.4 %all-to-all-start.1 = ((bf16[8,32,1024]{2,1,0:T(8,128)(2,1)}), bf16[8,32,1024]{2,1,0:T(8,128)(2,1)S(1)}, u32[]{:S(2)}, u32[]{:S(2)}) async-start(bf16[8,32,1024]{2,1,0:T(8,128)(2,1)} %broadcast_select_fusion.1), calls=%async_computation.1 | async-start | bytes 1048576 | tf_op jit(solution)/shard_map/all_to_all | solution.py:58
  233.8 13.0 %copy-start.1 = (bf16[1024,153]{0,1:T(8,128)(2,1)S(1)}, bf16[1024,153]{0,1:T(8,128)(2,1)}, u32[]{:S(2)}) copy-start(bf16[1024,153]{0,1:T(8,128)(2,1)} %param.30) | copy-start | bytes 940036
where the time goes:
time: 252 us; the launch traced here: 249 us
  matrix products  72.8 us (29%)
  waiting for transfers between devices  65.9 us (26%)
  local copies, waits for them, and re-layouts  42.9 us (17%)
  blocking collectives  42.2 us (17%)
  other arithmetic  14.1 us (6%)
  starting transfers between devices  11.2 us (4%)
    all_to_all x1, waiting for transfers between devices, local(): lax.all_to_all(outgoing, ('hst', 'dev'), split_axis=0, concat_axis=0, til...  53.6 us
    dot_general x1, matrix products, local(): jnp.dot(first_mean, neigh_first, preferred_element_type=jnp.float32)  49 us
    psum x1, blocking collectives, local(): lax.psum((jnp.sum(hidden_pre, axis=0), jnp.sum(hidden_pre * hidden_pre, a...  42.2 us
    gather x1, local copies, waits for them, and re-layouts, local(): hot_feat = jnp.take(hot_rows, hot_id, axis=0)  13.7 us
    dot_general x1, matrix products, local(): jnp.dot(second_mean, neigh_second, preferred_element_type=jnp.float32)  13 us
    gather x1, local copies, waits for them, and re-layouts, local(): cold_feat = jnp.take(arrived, cold_owner * slots + cold_pos, axis=0)  12.3 us
    all_to_all x1, waiting for transfers between devices, local(): lax.all_to_all(boundary, 'dev', split_axis=0, concat_axis=0, tiled=True)  12.3 us
    gather x1, local copies, waits for them, and re-layouts, local(): outgoing = jnp.take(cold_rows, cold_send[0], axis=0)  11.7 us
  transfers between devices with their start and end apart: 2, of which 2 were waited for; matrix products, arithmetic and copies ran while one was open for 6% of the time, Pallas kernels for 0%

commit v1 on v0

v1 whole, which is shorter than its diff:
```python
import functools

import jax
import jax.numpy as jnp
from jax import lax
from jax.experimental import pallas as pl
from jax.experimental.pallas import tpu as pltpu
from jax.sharding import PartitionSpec as P

epsilon = 1e-05
LANES = 128
GRANT = 48 * 1024 * 1024


def whole(shape):
    return pl.BlockSpec(shape, lambda *_: (0,) * len(shape))


def block_of(rows, wanted):
    while rows % wanted:
        wanted //= 2
    return wanted


def select_kernel(index_ref, rows_ref, out_ref):
    columns = lax.broadcasted_iota(jnp.int32, (index_ref.shape[0], rows_ref.shape[0]), 1)
    picks = jnp.where(index_ref[...] == columns, 1.0, 0.0).astype(jnp.bfloat16)
    out_ref[...] = jnp.dot(picks, rows_ref[...], preferred_element_type=jnp.float32).astype(out_ref.dtype)


def select_rows(rows, index):
    count, width = index.shape[0], rows.shape[1]
    step = block_of(count, 512)
    return pl.pallas_call(
        select_kernel,
        grid=(count // step,),
        in_specs=[pl.BlockSpec((step, 1), lambda i: (i, 0)), whole(rows.shape)],
        out_specs=pl.BlockSpec((step, width), lambda i: (i, 0)),
        out_shape=jax.ShapeDtypeStruct((count, width), rows.dtype),
        compiler_params=pltpu.CompilerParams(vmem_limit_bytes=GRANT),
        name="select_rows",
    )(index[:, None], rows)


def count_kernel(index_ref, out_ref):
    rows, fanout = index_ref.shape
    width = out_ref.shape[1]
    part = 16

    def some_rows(step, carry):
        here = pl.ds(pl.multiple_of(step * part, part), part)
        index = index_ref[here, :]
        lane = lax.broadcasted_iota(jnp.int32, (part, LANES), 1)
        spread = [jnp.broadcast_to(index[:, k : k + 1], (part, LANES)) for k in range(fanout)]
        for tile in range(width // LANES):
            columns = lane + tile * LANES
            total = jnp.zeros((part, LANES), jnp.float32)
            for k in range(fanout):
                total = total + jnp.where(spread[k] == columns, 1.0, 0.0)
            out_ref[here, tile * LANES : (tile + 1) * LANES] = total.astype(jnp.bfloat16)
        return carry

    lax.fori_loop(0, rows // part, some_rows, 0)


def count_matrix(index, width):
    rows, fanout = index.shape
    step = block_of(rows, 512)
    return pl.pallas_call(
        count_kernel,
        grid=(rows // step,),
        in_specs=[pl.BlockSpec((step, fanout), lambda i: (i, 0))],
        out_specs=pl.BlockSpec((step, width), lambda i: (i, 0)),
        out_shape=jax.ShapeDtypeStruct((rows, width), jnp.bfloat16),
        compiler_params=pltpu.CompilerParams(vmem_limit_bytes=16 * 1024 * 1024),
        cost_estimate=pl.CostEstimate(
            flops=rows * width * fanout * 150, bytes_accessed=rows * width * 2, transcendentals=0
        ),
        name="count_matrix",
    )(index)


def first_kernel(blocks, fanout, arrived_ref, place_ref, hot_ref, counts_ref, self_ref, neigh_ref,
                 pre_ref, stats_ref, features):
    step = pl.program_id(0)
    rows = place_ref.shape[0]

    @pl.when(step < blocks)
    def _():
        cold = jnp.dot(place_ref[...], arrived_ref[...], preferred_element_type=jnp.float32)
        here = pl.ds(pl.multiple_of(step * rows, rows), rows)
        features[here, :] = cold.astype(jnp.bfloat16) + hot_ref[...]

    @pl.when(step >= blocks)
    def _():
        here = pl.ds(pl.multiple_of((step - blocks) * rows, rows), rows)
        total = jnp.dot(counts_ref[...], features[...], preferred_element_type=jnp.float32)
        mean = (total / fanout).astype(jnp.bfloat16)
        pre = jnp.dot(features[here, :], self_ref[...], preferred_element_type=jnp.float32)
        pre = pre + jnp.dot(mean, neigh_ref[...], preferred_element_type=jnp.float32)
        pre_ref[...] = pre
        both = jnp.concatenate(
            [jnp.sum(pre, axis=0, keepdims=True), jnp.sum(pre * pre, axis=0, keepdims=True)], axis=0
        )

        @pl.when(step == blocks)
        def _():
            stats_ref[...] = both

        @pl.when(step > blocks)
        def _():
            stats_ref[...] += both


def first_layer(arrived, place, hot_feat, counts, self_first, neigh_first, fanout):
    nodes, width = hot_feat.shape
    units = self_first.shape[1]
    step = block_of(nodes, 512)
    blocks = nodes // step
    early = lambda i: (jnp.minimum(i, blocks - 1), 0)
    late = lambda i: (jnp.maximum(i - blocks, 0), 0)
    return pl.pallas_call(
        functools.partial(first_kernel, blocks, fanout),
        grid=(2 * blocks,),
        in_specs=[
            whole(arrived.shape),
            pl.BlockSpec((step, place.shape[1]), early),
            pl.BlockSpec((step, width), early),
            pl.BlockSpec((step, counts.shape[1]), late),
            whole(self_first.shape),
            whole(neigh_first.shape),
        ],
        out_specs=[pl.BlockSpec((step, units), late), whole((2, units))],
        out_shape=[
            jax.ShapeDtypeStruct((nodes, units), jnp.float32),
            jax.ShapeDtypeStruct((2, units), jnp.float32),
        ],
        scratch_shapes=[pltpu.VMEM((nodes, width), jnp.bfloat16)],
        compiler_params=pltpu.CompilerParams(vmem_limit_bytes=GRANT),
        name="first_layer",
    )(arrived, place, hot_feat, counts, self_first, neigh_first)


def stats_kernel(hosts, within, own_ref, out_ref, near, far, part, send_near, recv_near, send_far, recv_far):
    host, lane = lax.axis_index("hst"), lax.axis_index("dev")
    barrier = pltpu.get_barrier_semaphore()
    for away in range(1, within):
        pl.semaphore_signal(barrier, inc=1, device_id={"dev": lax.rem(lane + away, within)},
                            device_id_type=pl.DeviceIdType.MESH)
    for away in range(1, hosts):
        pl.semaphore_signal(barrier, inc=1, device_id={"hst": lax.rem(host + away, hosts)},
                            device_id_type=pl.DeviceIdType.MESH)
    pl.semaphore_wait(barrier, within + hosts - 2)

    def exchange(source, slots, axis, me, size, send, recv):
        copies = []
        for away in range(1, size):
            copy = pltpu.make_async_remote_copy(
                src_ref=source, dst_ref=slots.at[away - 1], send_sem=send.at[away - 1],
                recv_sem=recv.at[away - 1], device_id={axis: lax.rem(me + away, size)},
                device_id_type=pl.DeviceIdType.MESH,
            )
            copy.start()
            copies.append(copy)
        for copy in copies:
            copy.wait()
        total = source[...]
        for away in range(1, size):
            total = total + slots[away - 1]
        return total

    part[...] = exchange(own_ref, near, "dev", lane, within, send_near, recv_near)
    out_ref[...] = exchange(part, far, "hst", host, hosts, send_far, recv_far)


def sum_stats(own, hosts, within):
    return pl.pallas_call(
        functools.partial(stats_kernel, hosts, within),
        in_specs=[pl.BlockSpec(memory_space=pltpu.VMEM)],
        out_specs=pl.BlockSpec(memory_space=pltpu.VMEM),
        out_shape=jax.ShapeDtypeStruct(own.shape, own.dtype),
        scratch_shapes=[
            pltpu.VMEM((within - 1,) + own.shape, own.dtype),
            pltpu.VMEM((hosts - 1,) + own.shape, own.dtype),
            pltpu.VMEM(own.shape, own.dtype),
            pltpu.SemaphoreType.DMA((within - 1,)),
            pltpu.SemaphoreType.DMA((within - 1,)),
            pltpu.SemaphoreType.DMA((hosts - 1,)),
            pltpu.SemaphoreType.DMA((hosts - 1,)),
        ],
        compiler_params=pltpu.CompilerParams(collective_id=0, has_side_effects=True),
        name="sum_stats",
    )(own)


def norm_kernel(total_rows, pre_ref, stats_ref, gain_ref, shift_ref, picks_ref, hidden_ref, boundary_ref, held):
    step = pl.program_id(0)
    mean = stats_ref[0:1, :] / total_rows
    variance = stats_ref[1:2, :] / total_rows - mean * mean
    scale = lax.rsqrt(variance + epsilon)
    hidden = jnp.maximum((pre_ref[...] - mean) * scale * gain_ref[...] + shift_ref[...], 0.0)
    hidden = hidden.astype(jnp.bfloat16)
    hidden_ref[...] = hidden
    picked = jnp.dot(picks_ref[...], hidden, preferred_element_type=jnp.float32)

    @pl.when(step == 0)
    def _():
        held[...] = picked

    @pl.when(step > 0)
    def _():
        held[...] += picked

    @pl.when(step == pl.num_programs(0) - 1)
    def _():
        boundary_ref[...] = held[...].astype(jnp.bfloat16)


def norm_layer(pre, stats, gain, shift, picks, total_rows):
    nodes, units = pre.shape
    step = block_of(nodes, 512)
    edge = picks.shape[0]
    return pl.pallas_call(
        functools.partial(norm_kernel, total_rows),
        grid=(nodes // step,),
        in_specs=[
            pl.BlockSpec((step, units), lambda i: (i, 0)),
            whole(stats.shape),
            whole((1, units)),
            whole((1, units)),
            pl.BlockSpec((edge, step), lambda i: (0, i)),
        ],
        out_specs=[pl.BlockSpec((step, units), lambda i: (i, 0)), whole((edge, units))],
        out_shape=[
            jax.ShapeDtypeStruct((nodes, units), jnp.bfloat16),
            jax.ShapeDtypeStruct((edge, units), jnp.bfloat16),
        ],
        scratch_shapes=[pltpu.VMEM((edge, units), jnp.float32)],
        compiler_params=pltpu.CompilerParams(vmem_limit_bytes=GRANT),
        name="norm_layer",
    )(pre, stats, gain[None, :], shift[None, :], picks)


def last_kernel(within, fanout, boundary_ref, hidden_ref, counts_ref, self_ref, neigh_ref, out_ref,
                received, send, recv, own_sem):
    lane = lax.axis_index("dev")
    nodes = hidden_ref.shape[0]
    targets = counts_ref.shape[0]
    slots = boundary_ref.shape[0] // within
    barrier = pltpu.get_barrier_semaphore()
    for away in range(1, within):
        pl.semaphore_signal(barrier, inc=1, device_id={"dev": lax.rem(lane + away, within)},
                            device_id_type=pl.DeviceIdType.MESH)
    pl.semaphore_wait(barrier, within - 1)
    mine = pl.ds(pl.multiple_of(lane * slots, slots), slots)
    copies = []
    for away in range(1, within):
        peer = lax.rem(lane + away, within)
        copy = pltpu.make_async_remote_copy(
            src_ref=boundary_ref.at[pl.ds(pl.multiple_of(peer * slots, slots), slots)],
            dst_ref=received.at[mine],
            send_sem=send.at[away - 1], recv_sem=recv.at[away - 1], device_id={"dev": peer},
            device_id_type=pl.DeviceIdType.MESH,
        )
        copy.start()
        copies.append(copy)
    own = pltpu.make_async_copy(boundary_ref.at[mine], received.at[mine], own_sem)
    own.start()
    total = jnp.dot(counts_ref[:, :nodes], hidden_ref[...], preferred_element_type=jnp.float32)
    scores = jnp.dot(hidden_ref[:targets, :], self_ref[...], preferred_element_type=jnp.float32)
    own.wait()
    for copy in copies:
        copy.wait()
    total = total + jnp.dot(counts_ref[:, nodes:], received[...], preferred_element_type=jnp.float32)
    mean = (total / fanout).astype(jnp.bfloat16)
    out_ref[...] = scores + jnp.dot(mean, neigh_ref[...], preferred_element_type=jnp.float32)


def last_layer(boundary, hidden, counts, self_second, neigh_second, within, fanout):
    return pl.pallas_call(
        functools.partial(last_kernel, within, fanout),
        in_specs=[pl.BlockSpec(memory_space=pltpu.VMEM)] * 5,
        out_specs=pl.BlockSpec(memory_space=pltpu.VMEM),
        out_shape=jax.ShapeDtypeStruct((counts.shape[0], self_second.shape[1]), jnp.float32),
        scratch_shapes=[
            pltpu.VMEM(boundary.shape, boundary.dtype),
            pltpu.SemaphoreType.DMA((within - 1,)),
            pltpu.SemaphoreType.DMA((within - 1,)),
            pltpu.SemaphoreType.DMA,
        ],
        compiler_params=pltpu.CompilerParams(
            collective_id=1, has_side_effects=True, vmem_limit_bytes=GRANT
        ),
        name="last_layer",
    )(boundary, hidden, counts, self_second, neigh_second)


def local(
    hot_rows,
    cold_rows,
    hot_mask,
    hot_id,
    cold_owner,
    cold_pos,
    cold_send,
    adjacency_one,
    adjacency_two,
    halo_send,
    self_first,
    neigh_first,
    bn_gain,
    bn_shift,
    self_second,
    neigh_second,
):
    hosts = lax.axis_size("hst")
    within = lax.axis_size("dev")
    nodes = hot_mask.shape[0]
    outgoing = select_rows(cold_rows, cold_send[0])
    slots = outgoing.shape[0] // (hosts * within)
    arrived = lax.all_to_all(outgoing, ("hst", "dev"), split_axis=0, concat_axis=0, tiled=True)

    hot_feat = jnp.where(
        hot_mask[:, None] == 1, hot_rows.at[hot_id].get(mode="promise_in_bounds"), 0
    )
    source = jnp.where(hot_mask == 1, -1, cold_owner * slots + cold_pos)
    place = count_matrix(source[:, None], outgoing.shape[0])
    counts_one = count_matrix(adjacency_one, nodes)
    counts_two = count_matrix(adjacency_two, nodes + halo_send.shape[1])
    picks = count_matrix(halo_send[0][:, None], nodes)

    pre, own = first_layer(
        arrived, place, hot_feat, counts_one, self_first, neigh_first, adjacency_one.shape[1]
    )
    stats = sum_stats(own, hosts, within)
    hidden, boundary = norm_layer(pre, stats, bn_gain, bn_shift, picks, nodes * hosts * within)
    return last_layer(
        boundary, hidden, counts_two, self_second, neigh_second, within, adjacency_two.shape[1]
    )


def solution(mesh):
    placed = (
        P(),
        P(("hst", "dev"), None),
        P(("hst", "dev")),
        P(("hst", "dev")),
        P(("hst", "dev")),
        P(("hst", "dev")),
        P(("hst", "dev"), None),
        P(("hst", "dev"), None),
        P(("hst", "dev"), None),
        P(("hst", "dev"), None),
        P(),
        P(),
        P(),
        P(),
        P(),
        P(),
    )
    return jax.shard_map(
        local, mesh=mesh, in_specs=placed, out_specs=P(("hst", "dev"), None), check_vma=False
    )
```

time: 252 us -> 180 us (0.71)
  Pallas kernels: 0 us -> 136 us
  matrix products: 72.8 us -> 0 us
  waiting for transfers between devices: 65.9 us -> 0.01 us
  blocking collectives: 42.2 us -> 0 us
  other arithmetic: 14.1 us -> 1.95 us
  local copies, waits for them, and re-layouts: 42.9 us -> 34.5 us
  starting transfers between devices: 11.2 us -> 6.1 us
    pallas_call x0 -> x9, Pallas kernels: none -> 136 us  [the longest x4 60.8 us: count_matrix(): pl.pallas_call(count_kernel, grid=(rows // step,), in_specs=[pl.BlockSpec...]
    dot_general x4 -> x0, matrix products: 72.8 us -> none  [the longest x1 49 us: local(): jnp.dot(first_mean, neigh_first, preferred_element_type=jnp.float32)]
    all_to_all x1, waiting for transfers between devices: 53.6 us -> 0.01 us  [local(): lax.all_to_all(outgoing, ('hst', 'dev'), split_axis=0, concat_axis=0, til...]
    psum x1 -> x0, blocking collectives: 42.2 us -> none  [local(): lax.psum((jnp.sum(hidden_pre, axis=0), jnp.sum(hidden_pre * hidden_pre, a...]
    gather x4 -> x1, local copies, waits for them, and re-layouts: 42.1 us -> 13.7 us  [local(): hot_rows.at[hot_id].get(mode='promise_in_bounds')]
    unnamed x25 -> x52, local copies, waits for them, and re-layouts: 0.57 us -> 18.3 us
    all_to_all x1 -> x0, waiting for transfers between devices: 12.3 us -> none  [local(): lax.all_to_all(boundary, 'dev', split_axis=0, concat_axis=0, tiled=True)]
    convert_element_type x1 -> x0, other arithmetic: 6.94 us -> none  [local(): hidden = jax.nn.relu((hidden_pre - mean) * lax.rsqrt(variance + epsilon)...]
  transfers between devices with their start and end apart: 2 -> 1, of which waited for: 2 -> 0; matrix products, arithmetic and copies ran while one was open for 6% -> 11% of each run, Pallas kernels for 0% -> 34%
where the time goes in v1:
time: 180 us; the launch traced here: 179 us
  Pallas kernels  136 us (76%)
  local copies, waits for them, and re-layouts  34.5 us (19%)
  starting transfers between devices  6.1 us (3%)
  other arithmetic  1.95 us (1%)
    pallas_call x4, Pallas kernels, count_matrix(): pl.pallas_call(count_kernel, grid=(rows // step,), in_specs=[pl.BlockSpec...  60.8 us
    pallas_call x1, Pallas kernels, first_layer(): pl.pallas_call(functools.partial(first_kernel, blocks, fanout), grid=(2 *...  31.6 us
    pallas_call x1, Pallas kernels, last_layer(): pl.pallas_call(functools.partial(last_kernel, within, fanout), in_specs=[...  21.3 us
    unnamed x52, local copies, waits for them, and re-layouts  18.3 us
    gather x1, local copies, waits for them, and re-layouts, local(): hot_rows.at[hot_id].get(mode='promise_in_bounds')  13.7 us
    pallas_call x1, Pallas kernels, sum_stats(): pl.pallas_call(functools.partial(stats_kernel, hosts, within), in_specs=[...  11 us
    all_to_all x1, starting transfers between devices, local(): lax.all_to_all(outgoing, ('hst', 'dev'), split_axis=0, concat_axis=0, til...  6.1 us
    pallas_call x1, Pallas kernels, norm_layer(): pl.pallas_call(functools.partial(norm_kernel, total_rows), grid=(nodes //...  5.87 us
  transfers between devices with their start and end apart: 1, of which 0 were waited for; matrix products, arithmetic and copies ran while one was open for 11% of the time, Pallas kernels for 34%

profile of v1, /device:TPU:8, one launch (start us, length us, event | category | flops | bytes accessed | tf_op | source)
XLA Modules:
  0.0 178.8 jit_solution(17046660212538792755)
XLA Ops:
  0.0 1.1 copy.22.index_ref
  1.1 1.4 copy-done.7
  2.5 5.4 %select_rows.1 = bf16[2048,768]{1,0:T(8,128)(2,1)} custom-call(s32[2048,1]{1,0:T(8,128)S(1)} %copy.22.index_ref, bf16[1024,768]{1,0:T(8,128)(2,1)S(1)} %copy-done.7), custom_call_target="tpu_custom_call" | custom-call | tf_op jit(solution)/shard_map/select_rows/pallas_call | solution.py:34
  7.9 6.1 %all-to-all-start = ((bf16[32,64,768]{2,1,0:T(8,128)(2,1)}), bf16[32,64,768]{2,1,0:T(8,128)(2,1)}, u32[]{:S(2)}, u32[]{:S(2)}) async-start(bf16[32,64,768]{2,1,0:T(8,128)(2,1)} %bitcast.1), calls=%async_computation | async-start | bytes 6291456 | tf_op jit(solution)/shard_map/all_to_all | solution.py:321
  14.5 1.4 copy.24.index_ref
  16.0 0.9 copy.26.index_ref
  16.9 1.0 copy.27.self_ref
  17.9 1.0 copy.28.neigh_ref
  18.9 13.7 %gather_fusion = bf16[2048,768]{1,0:T(8,128)(2,1)} fusion(bf16[4096,768]{1,0:T(8,128)(2,1)} %param.16, s32[2048]{0:T(1024)S(1)} %fusion), kind=kCustom, calls=%fused_computation | custom fusion | bytes 6299648 | tf_op jit(solution)/shard_map/gather | solution.py:324
  32.6 1.3 count_matrix.6.picks_ref
  33.9 10.7 %count_matrix.4.place_ref = bf16[2048,2048]{1,0:T(8,128)(2,1)S(1)} custom-call(s32[2048,1]{1,0:T(8,128)S(1)} %copy.23.index_ref), custom_call_target="tpu_custom_call" | custom-call | flops 629145600 | bytes 8388608 | tf_op jit(solution)/shard_map/count_matrix/pallas_call | solution.py:69
  44.7 3.3 %copy-done = bf16[2048,2048]{1,0:T(8,128)(2,1)} copy-done((bf16[2048,2048]{1,0:T(8,128)(2,1)}, bf16[2048,2048]{1,0:T(8,128)(2,1)S(1)}, u32[]{:S(2)}) %copy-start) | copy-done | bytes 8388632
  47.9 10.8 %count_matrix.7.counts_ref = bf16[512,2304]{1,0:T(8,128)(2,1)S(1)} custom-call(s32[512,15]{1,0:T(8,128)S(1)} %copy-done.9), custom_call_target="tpu_custom_call" | custom-call | flops 2654208000 | bytes 2359296 | tf_op jit(solution)/shard_map/count_matrix/pallas_call | solution.py:69
  58.8 1.9 %broadcast_select_fusion.hot_ref = bf16[2048,768]{1,0:T(8,128)(2,1)} fusion(bf16[2048,768]{1,0:T(8,128)(2,1)S(1)} %copy-done.14, pred[2048]{0:T(1024)(128)(4,1)S(1)} %get-tuple-element.14), kind=kLoop, calls=%fused_computation.1 | loop fusion | flops 1572864 | bytes 6293504 | tf_op jit(solution)/shard_map/jit(_where)/select_n | solution.py:323
  60.7 38.0 %count_matrix.5.counts_ref = bf16[2048,2048]{1,0:T(8,128)(2,1)S(1)} custom-call(s32[2048,15]{1,0:T(8,128)S(1)} %copy-done.8), custom_call_target="tpu_custom_call" | custom-call | flops 9437184000 | bytes 8388608 | tf_op jit(solution)/shard_map/count_matrix/pallas_call | solution.py:69
  98.7 3.3 %copy-done.1 = bf16[2048,2048]{1,0:T(8,128)(2,1)} copy-done((bf16[2048,2048]{1,0:T(8,128)(2,1)}, bf16[2048,2048]{1,0:T(8,128)(2,1)S(1)}, u32[]{:S(2)}) %copy-start.1) | copy-done | bytes 8388632
  102.0 1.4 copy-done.5
  103.4 1.4 copy-done.6
  104.8 31.6 %first_layer.1 = (f32[2048,1024]{1,0:T(8,128)}, f32[2,1024]{1,0:T(2,128)S(1)}) custom-call(bf16[2048,768]{1,0:T(8,128)(2,1)} %bitcast.2.arrived_ref, bf16[2048,2048]{1,0:T(8,128)(2,1)} %copy-done, bf16[2048,768]{1,0:T(8,128)(2,1)} %broadcast_select_fusion.hot_ref, bf16[2048,2048]{1,0:T(8,128)(2,1)} %copy-done.1, bf16[768,1024]{1,0:T(8,128)(2,1)S(1)} %copy-done.5, ...), custom_call_target="tpu_custom_call" | custom-call | tf_op jit(solution)/shard_map/first_layer/pallas_call | solution.py:122
  137.0 11.0 %sum_stats.1.stats_ref = f32[2,1024]{1,0:T(2,128)} custom-call(f32[2,1024]{1,0:T(2,128)} %copy-done.11), custom_call_target="tpu_custom_call" | custom-call | tf_op jit(solution)/shard_map/sum_stats/pallas_call | solution.py:177
  148.7 5.9 %norm_layer.1 = (bf16[2048,1024]{1,0:T(8,128)(2,1)S(1)}, bf16[256,1024]{1,0:T(8,128)(2,1)S(1)}) custom-call(f32[2048,1024]{1,0:T(8,128)} %get-tuple-element.9.pre_ref, f32[2,1024]{1,0:T(2,128)S(1)} %copy-done.10, f32[1,1024]{1,0:T(1,128)S(1)} %bitcast.7, f32[1,1024]{1,0:T(1,128)S(1)} %bitcast.8, bf16[256,2048]{1,0:T(8,128)(2,1)S(1)} %count_matrix.6.picks_ref), custom_call_target="tpu_custom_call" | custom-call | tf_op jit(solution)/shard_map/norm_layer/pallas_call | solution.py:223
  154.6 1.9 %copy-done.2 = bf16[2048,1024]{1,0:T(8,128)(2,1)} copy-done((bf16[2048,1024]{1,0:T(8,128)(2,1)}, bf16[2048,1024]{1,0:T(8,128)(2,1)S(1)}, u32[]{:S(2)}) %copy-start.2) | copy-done | bytes 4194328
  156.6 21.3 %last_layer.1 = f32[512,153]{1,0:T(8,128)S(1)} custom-call(bf16[256,1024]{1,0:T(8,128)(2,1)S(1)} %get-tuple-element.11.boundary_ref, bf16[2048,1024]{1,0:T(8,128)(2,1)} %copy-done.2, bf16[512,2304]{1,0:T(8,128)(2,1)S(1)} %count_matrix.7.counts_ref, bf16[1024,153]{1,0:T(8,128)(2,1)S(1)} %copy-done.3, bf16[1024,153]{1,0:T(8,128)(2,1)S(1)} %copy-done.4), custom_call_target="tpu_custom_call" | custom-call | tf_op jit(solution)/shard_map/last_layer/pallas_call | solution.py:280
  177.9 0.9 copy.29
  (47 shorter events, 1.9 us)
Async XLA Ops:
  1.1 1.4 copy-start.7
  7.9 6.2 %copy-start.19 = (s32[2048]{0:T(1024)S(1)}, s32[2048]{0:T(1024)}, u32[]{:S(2)}) copy-start(s32[2048]{0:T(1024)} %param.21) | copy-start | bytes 24580
  7.9 6.2 %copy-start.20 = (s32[2048]{0:T(1024)S(1)}, s32[2048]{0:T(1024)}, u32[]{:S(2)}) copy-start(s32[2048]{0:T(1024)} %param.20) | copy-start | bytes 24580
  7.9 6.2 %copy-start.21 = (s32[2048]{0:T(1024)S(1)}, s32[2048]{0:T(1024)}, u32[]{:S(2)}) copy-start(s32[2048]{0:T(1024)} %param.18) | copy-start | bytes 24580
  7.9 6.6 %copy-start.17 = (s32[2048,15]{0,1:T(8,128)S(1)}, s32[2048,15]{0,1:T(8,128)}, u32[]{:S(2)}) copy-start(s32[2048,15]{0,1:T(8,128)} %param.23) | copy-start | bytes 368644
  7.9 8.0 %copy-start.23 = (s32[1,256]{1,0:T(1,128)S(1)}, s32[1,256]{1,0:T(1,128)}, u32[]{:S(2)}) copy-start(s32[1,256]{1,0:T(1,128)} %param.25) | copy-start | bytes 3076
  7.9 8.1 %copy-start.18 = (s32[512,15]{0,1:T(8,128)S(1)}, s32[512,15]{0,1:T(8,128)}, u32[]{:S(2)}) copy-start(s32[512,15]{0,1:T(8,128)} %param.24) | copy-start | bytes 92164
  7.9 9.0 %copy-start.15 = (bf16[1024,153]{0,1:T(8,128)(2,1)S(1)}, bf16[1024,153]{0,1:T(8,128)(2,1)}, u32[]{:S(2)}) copy-start(bf16[1024,153]{0,1:T(8,128)(2,1)} %param.30) | copy-start | bytes 940036
  7.9 94.0 %all-to-all-start = ((bf16[32,64,768]{2,1,0:T(8,128)(2,1)}), bf16[32,64,768]{2,1,0:T(8,128)(2,1)}, u32[]{:S(2)}, u32[]{:S(2)}) async-start(bf16[32,64,768]{2,1,0:T(8,128)(2,1)} %bitcast.1), calls=%async_computation | async-start | bytes 6291456 | tf_op jit(solution)/shard_map/all_to_all | solution.py:321
  14.0 3.8 %copy-start.16 = (bf16[1024,153]{0,1:T(8,128)(2,1)S(1)}, bf16[1024,153]{0,1:T(8,128)(2,1)}, u32[]{:S(2)}) copy-start(bf16[1024,153]{0,1:T(8,128)(2,1)} %param.31) | copy-start | bytes 940036
  14.1 4.8 %copy-start.22 = (s32[2048]{0:T(1024)S(1)}, s32[2048]{0:T(1024)}, u32[]{:S(2)}) copy-start(s32[2048]{0:T(1024)} %param.19) | copy-start | bytes 24580
  33.9 14.0 %copy-start.9 = (s32[512,15]{1,0:T(8,128)S(1)}, s32[512,15]{1,0:T(8,128)}, u32[]{:S(2)}) copy-start(s32[512,15]{1,0:T(8,128)} %copy.26.index_ref) | copy-start | bytes 92164
  44.6 3.3 %copy-start = (bf16[2048,2048]{1,0:T(8,128)(2,1)}, bf16[2048,2048]{1,0:T(8,128)(2,1)S(1)}, u32[]{:S(2)}) copy-start(bf16[2048,2048]{1,0:T(8,128)(2,1)S(1)} %count_matrix.4.place_ref) | copy-start | bytes 25165828
  47.9 10.8 %copy-start.14 = (bf16[2048,768]{1,0:T(8,128)(2,1)S(1)}, bf16[2048,768]{1,0:T(8,128)(2,1)}, u32[]{:S(2)}) copy-start(bf16[2048,768]{1,0:T(8,128)(2,1)} %gather_fusion) | copy-start | bytes 9437188
  58.7 1.9 %copy-start.8 = (s32[2048,15]{1,0:T(8,128)S(1)}, s32[2048,15]{1,0:T(8,128)}, u32[]{:S(2)}) copy-start(s32[2048,15]{1,0:T(8,128)} %copy.24.index_ref) | copy-start | bytes 368644
  98.7 3.3 %copy-start.1 = (bf16[2048,2048]{1,0:T(8,128)(2,1)}, bf16[2048,2048]{1,0:T(8,128)(2,1)S(1)}, u32[]{:S(2)}) copy-start(bf16[2048,2048]{1,0:T(8,128)(2,1)S(1)} %count_matrix.5.counts_ref) | copy-start | bytes 25165828
  102.0 1.4 copy-start.5
  103.4 1.4 copy-start.6
  104.8 43.2 %copy-start.12 = (f32[1024]{0:T(1024)S(1)}, f32[1024]{0:T(1024)}, u32[]{:S(2)}) copy-start(f32[1024]{0:T(1024)} %param.28) | copy-start | bytes 12292
  104.8 43.3 %copy-start.13 = (f32[1024]{0:T(1024)S(1)}, f32[1024]{0:T(1024)}, u32[]{:S(2)}) copy-start(f32[1024]{0:T(1024)} %param.29) | copy-start | bytes 12292
  148.0 0.7 copy-start.10
  148.7 7.8 %copy-start.3 = (bf16[1024,153]{1,0:T(8,128)(2,1)S(1)}, bf16[1024,153]{1,0:T(8,128)(2,1)}, u32[]{:S(2)}) copy-start(bf16[1024,153]{1,0:T(8,128)(2,1)} %copy.27.self_ref) | copy-start | bytes 940036
  148.7 7.8 %copy-start.4 = (bf16[1024,153]{1,0:T(8,128)(2,1)S(1)}, bf16[1024,153]{1,0:T(8,128)(2,1)}, u32[]{:S(2)}) copy-start(bf16[1024,153]{1,0:T(8,128)(2,1)} %copy.28.neigh_ref) | copy-start | bytes 940036
  154.6 1.9 %copy-start.2 = (bf16[2048,1024]{1,0:T(8,128)(2,1)}, bf16[2048,1024]{1,0:T(8,128)(2,1)S(1)}, u32[]{:S(2)}) copy-start(bf16[2048,1024]{1,0:T(8,128)(2,1)S(1)} %get-tuple-element.12.hidden_ref) | copy-start | bytes 12582916
  (1 other events, 0.6 us)

commit v2 on v1

--- a/solution.py
+++ b/solution.py
@@ -22,9 +22,13 @@
     return wanted
 
 
+def one_hot(index, width):
+    columns = lax.broadcasted_iota(jnp.int32, (index.shape[0], width), 1)
+    return jnp.where(index == columns, 1.0, 0.0).astype(jnp.bfloat16)
+
+
 def select_kernel(index_ref, rows_ref, out_ref):
-    columns = lax.broadcasted_iota(jnp.int32, (index_ref.shape[0], rows_ref.shape[0]), 1)
-    picks = jnp.where(index_ref[...] == columns, 1.0, 0.0).astype(jnp.bfloat16)
+    picks = one_hot(index_ref[...], rows_ref.shape[0])
     out_ref[...] = jnp.dot(picks, rows_ref[...], preferred_element_type=jnp.float32).astype(out_ref.dtype)
 
 
@@ -50,14 +54,17 @@
     def some_rows(step, carry):
         here = pl.ds(pl.multiple_of(step * part, part), part)
         index = index_ref[here, :]
-        lane = lax.broadcasted_iota(jnp.int32, (part, LANES), 1)
-        spread = [jnp.broadcast_to(index[:, k : k + 1], (part, LANES)) for k in range(fanout)]
+        lane = lax.broadcasted_iota(jnp.int32, (part, LANES), 1).astype(jnp.int16)
+        spread = [
+            jnp.broadcast_to(index[:, k : k + 1], (part, LANES)).astype(jnp.int16) for k in range(fanout)
+        ]
+        one, none = jnp.ones((part, LANES), jnp.bfloat16), jnp.zeros((part, LANES), jnp.bfloat16)
         for tile in range(width // LANES):
-            columns = lane + tile * LANES
-            total = jnp.zeros((part, LANES), jnp.float32)
+            columns = lane + jnp.int16(tile * LANES)
+            total = none
             for k in range(fanout):
-                total = total + jnp.where(spread[k] == columns, 1.0, 0.0)
-            out_ref[here, tile * LANES : (tile + 1) * LANES] = total.astype(jnp.bfloat16)
+                total = total + jnp.where(spread[k] == columns, one, none)
+            out_ref[here, tile * LANES : (tile + 1) * LANES] = total
         return carry
 
     lax.fori_loop(0, rows // part, some_rows, 0)
@@ -74,7 +81,7 @@
         out_shape=jax.ShapeDtypeStruct((rows, width), jnp.bfloat16),
         compiler_params=pltpu.CompilerParams(vmem_limit_bytes=16 * 1024 * 1024),
         cost_estimate=pl.CostEstimate(
-            flops=rows * width * fanout * 150, bytes_accessed=rows * width * 2, transcendentals=0
+            flops=rows * width * fanout * 100, bytes_accessed=rows * width * 2, transcendentals=0
         ),
         name="count_matrix",
     )(index)
@@ -87,7 +94,8 @@
 
     @pl.when(step < blocks)
     def _():
-        cold = jnp.dot(place_ref[...], arrived_ref[...], preferred_element_type=jnp.float32)
+        place = one_hot(place_ref[...], arrived_ref.shape[0])
+        cold = jnp.dot(place, arrived_ref[...], preferred_element_type=jnp.float32)
         here = pl.ds(pl.multiple_of(step * rows, rows), rows)
         features[here, :] = cold.astype(jnp.bfloat16) + hot_ref[...]
 
@@ -201,7 +209,8 @@
     hidden = jnp.maximum((pre_ref[...] - mean) * scale * gain_ref[...] + shift_ref[...], 0.0)
     hidden = hidden.astype(jnp.bfloat16)
     hidden_ref[...] = hidden
-    picked = jnp.dot(picks_ref[...], hidden, preferred_element_type=jnp.float32)
+    picks = one_hot(picks_ref[...] - step * hidden.shape[0], hidden.shape[0])
+    picked = jnp.dot(picks, hidden, preferred_element_type=jnp.float32)
 
     @pl.when(step == 0)
     def _():
@@ -228,7 +237,7 @@
             whole(stats.shape),
             whole((1, units)),
             whole((1, units)),
-            pl.BlockSpec((edge, step), lambda i: (0, i)),
+            whole((edge, 1)),
         ],
         out_specs=[pl.BlockSpec((step, units), lambda i: (i, 0)), whole((edge, units))],
         out_shape=[
@@ -324,10 +333,10 @@
         hot_mask[:, None] == 1, hot_rows.at[hot_id].get(mode="promise_in_bounds"), 0
     )
     source = jnp.where(hot_mask == 1, -1, cold_owner * slots + cold_pos)
-    place = count_matrix(source[:, None], outgoing.shape[0])
+    place = source[:, None]
     counts_one = count_matrix(adjacency_one, nodes)
     counts_two = count_matrix(adjacency_two, nodes + halo_send.shape[1])
-    picks = count_matrix(halo_send[0][:, None], nodes)
+    picks = halo_send[0][:, None]
 
     pre, own = first_layer(
         arrived, place, hot_feat, counts_one, self_first, neigh_first, adjacency_one.shape[1]

time: 180 us -> 161 us (0.89)
  Pallas kernels: 136 us -> 105 us
  waiting for transfers between devices: 0.01 us -> 15.3 us
  local copies, waits for them, and re-layouts: 34.5 us -> 32.1 us
    pallas_call x4 -> x2, Pallas kernels: 60.8 us -> 28.4 us  [count_matrix(): pl.pallas_call(count_kernel, grid=(rows // step,), in_specs=[pl.BlockSpec...]
    all_to_all x1, waiting for transfers between devices: 0.01 us -> 15.3 us  [local(): lax.all_to_all(outgoing, ('hst', 'dev'), split_axis=0, concat_axis=0, til...]
    unnamed x52 -> x50, local copies, waits for them, and re-layouts: 18.3 us -> 16 us
    pallas_call x1, Pallas kernels: 11 us -> 13.2 us  [sum_stats(): pl.pallas_call(functools.partial(stats_kernel, hosts, within), in_specs=[...]
  transfers between devices with their start and end apart: 1 -> 1, of which waited for: 0 -> 1; matrix products, arithmetic and copies ran while one was open for 11% -> 13% of each run, Pallas kernels for 34% -> 18%
where the time goes in v2:
time: 161 us
  Pallas kernels  105 us (65%)
  local copies, waits for them, and re-layouts  32.1 us (20%)
  waiting for transfers between devices  15.3 us (10%)
  starting transfers between devices  6.1 us (4%)
  other arithmetic  1.89 us (1%)
    pallas_call x1, Pallas kernels, first_layer(): pl.pallas_call(functools.partial(first_kernel, blocks, fanout), grid=(2 *...  30.9 us
    pallas_call x2, Pallas kernels, count_matrix(): pl.pallas_call(count_kernel, grid=(rows // step,), in_specs=[pl.BlockSpec...  28.4 us
    pallas_call x1, Pallas kernels, last_layer(): pl.pallas_call(functools.partial(last_kernel, within, fanout), in_specs=[...  21.3 us
    unnamed x50, local copies, waits for them, and re-layouts  16 us
    all_to_all x1, waiting for transfers between devices, local(): lax.all_to_all(outgoing, ('hst', 'dev'), split_axis=0, concat_axis=0, til...  15.3 us
    gather x1, local copies, waits for them, and re-layouts, local(): hot_rows.at[hot_id].get(mode='promise_in_bounds')  13.7 us
    pallas_call x1, Pallas kernels, sum_stats(): pl.pallas_call(functools.partial(stats_kernel, hosts, within), in_specs=[...  13.2 us
    all_to_all x1, starting transfers between devices, local(): lax.all_to_all(outgoing, ('hst', 'dev'), split_axis=0, concat_axis=0, til...  6.1 us
  transfers between devices with their start and end apart: 1, of which 1 were waited for; matrix products, arithmetic and copies ran while one was open for 13% of the time, Pallas kernels for 18%

profile of v2, /device:TPU:8, one launch (start us, length us, event | category | flops | bytes accessed | tf_op | source)
XLA Modules:
  0.0 160.7 jit_solution(2795435296358168756)
XLA Ops:
  0.0 1.1 copy.22.index_ref
  1.1 1.4 copy-done.6
  2.5 5.4 %select_rows.1 = bf16[2048,768]{1,0:T(8,128)(2,1)} custom-call(s32[2048,1]{1,0:T(8,128)S(1)} %copy.22.index_ref, bf16[1024,768]{1,0:T(8,128)(2,1)S(1)} %copy-done.6), custom_call_target="tpu_custom_call" | custom-call | tf_op jit(solution)/shard_map/select_rows/pallas_call | solution.py:38
  7.9 6.1 %all-to-all-start = ((bf16[32,64,768]{2,1,0:T(8,128)(2,1)}), bf16[32,64,768]{2,1,0:T(8,128)(2,1)}, u32[]{:S(2)}, u32[]{:S(2)}) async-start(bf16[32,64,768]{2,1,0:T(8,128)(2,1)} %bitcast.1), calls=%async_computation | async-start | bytes 6291456 | tf_op jit(solution)/shard_map/all_to_all | solution.py:330
  14.5 1.4 copy.23.index_ref
  16.0 0.9 copy.26.index_ref
  16.9 1.0 copy.27.self_ref
  17.9 1.0 copy.28.neigh_ref
  18.9 13.7 %gather_fusion = bf16[2048,768]{1,0:T(8,128)(2,1)} fusion(bf16[4096,768]{1,0:T(8,128)(2,1)} %param.16, s32[2048]{0:T(1024)S(1)} %fusion), kind=kCustom, calls=%fused_computation | custom fusion | bytes 6299648 | tf_op jit(solution)/shard_map/gather | solution.py:333
  32.5 0.9 copy-done.8
  33.5 6.0 %count_matrix.3.counts_ref = bf16[512,2304]{1,0:T(8,128)(2,1)S(1)} custom-call(s32[512,15]{1,0:T(8,128)S(1)} %copy-done.8), custom_call_target="tpu_custom_call" | custom-call | flops 1769472000 | bytes 2359296 | tf_op jit(solution)/shard_map/count_matrix/pallas_call | solution.py:76
  39.5 22.4 %count_matrix.2.counts_ref = bf16[2048,2048]{1,0:T(8,128)(2,1)S(1)} custom-call(s32[2048,15]{1,0:T(8,128)S(1)} %copy-done.7), custom_call_target="tpu_custom_call" | custom-call | flops 6291456000 | bytes 8388608 | tf_op jit(solution)/shard_map/count_matrix/pallas_call | solution.py:76
  61.9 3.3 %copy-done = bf16[2048,2048]{1,0:T(8,128)(2,1)} copy-done((bf16[2048,2048]{1,0:T(8,128)(2,1)}, bf16[2048,2048]{1,0:T(8,128)(2,1)S(1)}, u32[]{:S(2)}) %copy-start) | copy-done | bytes 8388632
  65.2 1.9 %broadcast_select_fusion.hot_ref = bf16[2048,768]{1,0:T(8,128)(2,1)} fusion(bf16[2048,768]{1,0:T(8,128)(2,1)S(1)} %copy-done.13, pred[2048]{0:T(1024)(128)(4,1)S(1)} %get-tuple-element.14), kind=kLoop, calls=%fused_computation.1 | loop fusion | flops 1572864 | bytes 6293504 | tf_op jit(solution)/shard_map/jit(_where)/select_n | solution.py:332
  67.1 15.3 %all-to-all-done = bf16[32,64,768]{2,1,0:T(8,128)(2,1)} async-done(((bf16[32,64,768]{2,1,0:T(8,128)(2,1)}), bf16[32,64,768]{2,1,0:T(8,128)(2,1)}, u32[]{:S(2)}, u32[]{:S(2)}) %all-to-all-start) | async-done | bytes 3145760 | tf_op jit(solution)/shard_map/all_to_all | solution.py:330
  82.4 1.4 copy-done.4
  83.8 1.4 copy-done.5
  85.2 30.9 %first_layer.1 = (f32[2048,1024]{1,0:T(8,128)}, f32[2,1024]{1,0:T(2,128)S(1)}) custom-call(bf16[2048,768]{1,0:T(8,128)(2,1)} %bitcast.2.arrived_ref, s32[2048,1]{1,0:T(8,128)S(1)} %copy.24.place_ref, bf16[2048,768]{1,0:T(8,128)(2,1)} %broadcast_select_fusion.hot_ref, bf16[2048,2048]{1,0:T(8,128)(2,1)} %copy-done, bf16[768,1024]{1,0:T(8,128)(2,1)S(1)} %copy-done.4, ...), custom_call_target="tpu_custom_call" | custom-call | tf_op jit(solution)/shard_map/first_layer/pallas_call | solution.py:130
  116.6 13.2 %sum_stats.1.stats_ref = f32[2,1024]{1,0:T(2,128)} custom-call(f32[2,1024]{1,0:T(2,128)} %copy-done.10), custom_call_target="tpu_custom_call" | custom-call | tf_op jit(solution)/shard_map/sum_stats/pallas_call | solution.py:185
  129.9 0.7 copy-done.9
  130.6 5.9 %norm_layer.1 = (bf16[2048,1024]{1,0:T(8,128)(2,1)S(1)}, bf16[256,1024]{1,0:T(8,128)(2,1)S(1)}) custom-call(f32[2048,1024]{1,0:T(8,128)} %get-tuple-element.9.pre_ref, f32[2,1024]{1,0:T(2,128)S(1)} %copy-done.9, f32[1,1024]{1,0:T(1,128)S(1)} %bitcast.7, f32[1,1024]{1,0:T(1,128)S(1)} %bitcast.8, s32[256,1]{1,0:T(8,128)S(1)} %copy.25.picks_ref), custom_call_target="tpu_custom_call" | custom-call | tf_op jit(solution)/shard_map/norm_layer/pallas_call | solution.py:232
  136.5 1.9 %copy-done.1 = bf16[2048,1024]{1,0:T(8,128)(2,1)} copy-done((bf16[2048,1024]{1,0:T(8,128)(2,1)}, bf16[2048,1024]{1,0:T(8,128)(2,1)S(1)}, u32[]{:S(2)}) %copy-start.1) | copy-done | bytes 4194328
  138.4 21.3 %last_layer.1 = f32[512,153]{1,0:T(8,128)S(1)} custom-call(bf16[256,1024]{1,0:T(8,128)(2,1)S(1)} %get-tuple-element.11.boundary_ref, bf16[2048,1024]{1,0:T(8,128)(2,1)} %copy-done.1, bf16[512,2304]{1,0:T(8,128)(2,1)S(1)} %count_matrix.3.counts_ref, bf16[1024,153]{1,0:T(8,128)(2,1)S(1)} %copy-done.2, bf16[1024,153]{1,0:T(8,128)(2,1)S(1)} %copy-done.3), custom_call_target="tpu_custom_call" | custom-call | tf_op jit(solution)/shard_map/last_layer/pallas_call | solution.py:289
  159.8 0.9 copy.29
  (43 shorter events, 1.2 us)
Async XLA Ops:
  1.1 1.4 copy-start.6
  7.9 6.2 %copy-start.18 = (s32[2048]{0:T(1024)S(1)}, s32[2048]{0:T(1024)}, u32[]{:S(2)}) copy-start(s32[2048]{0:T(1024)} %param.21) | copy-start | bytes 24580
  7.9 6.2 %copy-start.19 = (s32[2048]{0:T(1024)S(1)}, s32[2048]{0:T(1024)}, u32[]{:S(2)}) copy-start(s32[2048]{0:T(1024)} %param.20) | copy-start | bytes 24580
  7.9 6.2 %copy-start.20 = (s32[2048]{0:T(1024)S(1)}, s32[2048]{0:T(1024)}, u32[]{:S(2)}) copy-start(s32[2048]{0:T(1024)} %param.18) | copy-start | bytes 24580
  7.9 6.6 %copy-start.16 = (s32[2048,15]{0,1:T(8,128)S(1)}, s32[2048,15]{0,1:T(8,128)}, u32[]{:S(2)}) copy-start(s32[2048,15]{0,1:T(8,128)} %param.23) | copy-start | bytes 368644
  7.9 8.0 %copy-start.22 = (s32[1,256]{1,0:T(1,128)S(1)}, s32[1,256]{1,0:T(1,128)}, u32[]{:S(2)}) copy-start(s32[1,256]{1,0:T(1,128)} %param.25) | copy-start | bytes 3076
  7.9 8.1 %copy-start.17 = (s32[512,15]{0,1:T(8,128)S(1)}, s32[512,15]{0,1:T(8,128)}, u32[]{:S(2)}) copy-start(s32[512,15]{0,1:T(8,128)} %param.24) | copy-start | bytes 92164
  7.9 9.0 %copy-start.14 = (bf16[1024,153]{0,1:T(8,128)(2,1)S(1)}, bf16[1024,153]{0,1:T(8,128)(2,1)}, u32[]{:S(2)}) copy-start(bf16[1024,153]{0,1:T(8,128)(2,1)} %param.30) | copy-start | bytes 940036
  7.9 74.4 %all-to-all-start = ((bf16[32,64,768]{2,1,0:T(8,128)(2,1)}), bf16[32,64,768]{2,1,0:T(8,128)(2,1)}, u32[]{:S(2)}, u32[]{:S(2)}) async-start(bf16[32,64,768]{2,1,0:T(8,128)(2,1)} %bitcast.1), calls=%async_computation | async-start | bytes 6291456 | tf_op jit(solution)/shard_map/all_to_all | solution.py:330
  14.0 3.8 %copy-start.15 = (bf16[1024,153]{0,1:T(8,128)(2,1)S(1)}, bf16[1024,153]{0,1:T(8,128)(2,1)}, u32[]{:S(2)}) copy-start(bf16[1024,153]{0,1:T(8,128)(2,1)} %param.31) | copy-start | bytes 940036
  14.1 4.8 %copy-start.21 = (s32[2048]{0:T(1024)S(1)}, s32[2048]{0:T(1024)}, u32[]{:S(2)}) copy-start(s32[2048]{0:T(1024)} %param.19) | copy-start | bytes 24580
  32.5 0.9 copy-start.8
  33.5 6.0 %copy-start.7 = (s32[2048,15]{1,0:T(8,128)S(1)}, s32[2048,15]{1,0:T(8,128)}, u32[]{:S(2)}) copy-start(s32[2048,15]{1,0:T(8,128)} %copy.23.index_ref) | copy-start | bytes 368644
  39.5 25.7 %copy-start.13 = (bf16[2048,768]{1,0:T(8,128)(2,1)S(1)}, bf16[2048,768]{1,0:T(8,128)(2,1)}, u32[]{:S(2)}) copy-start(bf16[2048,768]{1,0:T(8,128)(2,1)} %gather_fusion) | copy-start | bytes 9437188
  61.9 3.3 %copy-start = (bf16[2048,2048]{1,0:T(8,128)(2,1)}, bf16[2048,2048]{1,0:T(8,128)(2,1)S(1)}, u32[]{:S(2)}) copy-start(bf16[2048,2048]{1,0:T(8,128)(2,1)S(1)} %count_matrix.2.counts_ref) | copy-start | bytes 25165828
  82.4 1.4 copy-start.4
  83.8 1.4 copy-start.5
  85.2 44.7 %copy-start.11 = (f32[1024]{0:T(1024)S(1)}, f32[1024]{0:T(1024)}, u32[]{:S(2)}) copy-start(f32[1024]{0:T(1024)} %param.28) | copy-start | bytes 12292
  85.2 44.7 %copy-start.12 = (f32[1024]{0:T(1024)S(1)}, f32[1024]{0:T(1024)}, u32[]{:S(2)}) copy-start(f32[1024]{0:T(1024)} %param.29) | copy-start | bytes 12292
  116.0 0.6 copy-start.10
  129.9 0.7 copy-start.9
  130.6 7.9 %copy-start.2 = (bf16[1024,153]{1,0:T(8,128)(2,1)S(1)}, bf16[1024,153]{1,0:T(8,128)(2,1)}, u32[]{:S(2)}) copy-start(bf16[1024,153]{1,0:T(8,128)(2,1)} %copy.27.self_ref) | copy-start | bytes 940036
  130.6 7.9 %copy-start.3 = (bf16[1024,153]{1,0:T(8,128)(2,1)S(1)}, bf16[1024,153]{1,0:T(8,128)(2,1)}, u32[]{:S(2)}) copy-start(bf16[1024,153]{1,0:T(8,128)(2,1)} %copy.28.neigh_ref) | copy-start | bytes 940036
  136.5 2.0 %copy-start.1 = (bf16[2048,1024]{1,0:T(8,128)(2,1)}, bf16[2048,1024]{1,0:T(8,128)(2,1)S(1)}, u32[]{:S(2)}) copy-start(bf16[2048,1024]{1,0:T(8,128)(2,1)S(1)} %get-tuple-element.12.hidden_ref) | copy-start | bytes 12582916

commit v3 on v2

--- a/solution.py
+++ b/solution.py
@@ -9,7 +9,7 @@
 
 epsilon = 1e-05
 LANES = 128
-GRANT = 48 * 1024 * 1024
+MIB = 1024 * 1024
 
 
 def whole(shape):
@@ -41,7 +41,7 @@
         in_specs=[pl.BlockSpec((step, 1), lambda i: (i, 0)), whole(rows.shape)],
         out_specs=pl.BlockSpec((step, width), lambda i: (i, 0)),
         out_shape=jax.ShapeDtypeStruct((count, width), rows.dtype),
-        compiler_params=pltpu.CompilerParams(vmem_limit_bytes=GRANT),
+        compiler_params=pltpu.CompilerParams(vmem_limit_bytes=16 * MIB),
         name="select_rows",
     )(index[:, None], rows)
 
@@ -79,7 +79,7 @@
         in_specs=[pl.BlockSpec((step, fanout), lambda i: (i, 0))],
         out_specs=pl.BlockSpec((step, width), lambda i: (i, 0)),
         out_shape=jax.ShapeDtypeStruct((rows, width), jnp.bfloat16),
-        compiler_params=pltpu.CompilerParams(vmem_limit_bytes=16 * 1024 * 1024),
+        compiler_params=pltpu.CompilerParams(vmem_limit_bytes=16 * MIB),
         cost_estimate=pl.CostEstimate(
             flops=rows * width * fanout * 100, bytes_accessed=rows * width * 2, transcendentals=0
         ),
@@ -144,7 +144,7 @@
             jax.ShapeDtypeStruct((2, units), jnp.float32),
         ],
         scratch_shapes=[pltpu.VMEM((nodes, width), jnp.bfloat16)],
-        compiler_params=pltpu.CompilerParams(vmem_limit_bytes=GRANT),
+        compiler_params=pltpu.CompilerParams(vmem_limit_bytes=36 * MIB),
         name="first_layer",
     )(arrived, place, hot_feat, counts, self_first, neigh_first)
 
@@ -196,7 +196,9 @@
             pltpu.SemaphoreType.DMA((hosts - 1,)),
             pltpu.SemaphoreType.DMA((hosts - 1,)),
         ],
-        compiler_params=pltpu.CompilerParams(collective_id=0, has_side_effects=True),
+        compiler_params=pltpu.CompilerParams(
+            collective_id=0, has_side_effects=True, vmem_limit_bytes=4 * MIB
+        ),
         name="sum_stats",
     )(own)
 
@@ -245,7 +247,7 @@
             jax.ShapeDtypeStruct((edge, units), jnp.bfloat16),
         ],
         scratch_shapes=[pltpu.VMEM((edge, units), jnp.float32)],
-        compiler_params=pltpu.CompilerParams(vmem_limit_bytes=GRANT),
+        compiler_params=pltpu.CompilerParams(vmem_limit_bytes=20 * MIB),
         name="norm_layer",
     )(pre, stats, gain[None, :], shift[None, :], picks)
 
@@ -298,7 +300,7 @@
             pltpu.SemaphoreType.DMA,
         ],
         compiler_params=pltpu.CompilerParams(
-            collective_id=1, has_side_effects=True, vmem_limit_bytes=GRANT
+            collective_id=1, has_side_effects=True, vmem_limit_bytes=24 * MIB
         ),
         name="last_layer",
     )(boundary, hidden, counts, self_second, neigh_second)

time: 161 us -> 158 us (0.981)
  local copies, waits for them, and re-layouts: 32.1 us -> 40.5 us
  Pallas kernels: 105 us -> 96.9 us
  waiting for transfers between devices: 15.3 us -> 11.1 us
    unnamed x50 -> x46, local copies, waits for them, and re-layouts: 16 us -> 23.3 us
    all_to_all x1, waiting for transfers between devices: 15.3 us -> 11.1 us  [local(): lax.all_to_all(outgoing, ('hst', 'dev'), split_axis=0, concat_axis=0, til...]
    pallas_call x1, Pallas kernels: 5.89 us -> 3.24 us  [norm_layer(): pl.pallas_call(functools.partial(norm_kernel, total_rows), grid=(nodes //...]
    pallas_call x1, Pallas kernels: 21.3 us -> 19.3 us  [last_layer(): pl.pallas_call(functools.partial(last_kernel, within, fanout), in_specs=[...]
  transfers between devices with their start and end apart: 1 -> 1, of which waited for: 1 -> 1; matrix products, arithmetic and copies ran while one was open for 13% -> 15% of each run, Pallas kernels for 18% -> 18%
where the time goes in v3:
time: 158 us; the launch traced here: 157 us
  Pallas kernels  96.9 us (61%)
  local copies, waits for them, and re-layouts  40.5 us (26%)
  waiting for transfers between devices  11.1 us (7%)
  starting transfers between devices  6.05 us (4%)
  other arithmetic  2.64 us (2%)
    pallas_call x1, Pallas kernels, first_layer(): pl.pallas_call(functools.partial(first_kernel, blocks, fanout), grid=(2 *...  29.6 us
    pallas_call x2, Pallas kernels, count_matrix(): pl.pallas_call(count_kernel, grid=(rows // step,), in_specs=[pl.BlockSpec...  28.4 us
    unnamed x46, local copies, waits for them, and re-layouts  23.3 us
    pallas_call x1, Pallas kernels, last_layer(): pl.pallas_call(functools.partial(last_kernel, within, fanout), in_specs=[...  19.3 us
    gather x1, local copies, waits for them, and re-layouts, local(): hot_rows.at[hot_id].get(mode='promise_in_bounds')  13.7 us
    pallas_call x1, Pallas kernels, sum_stats(): pl.pallas_call(functools.partial(stats_kernel, hosts, within), in_specs=[...  11.9 us
    all_to_all x1, waiting for transfers between devices, local(): lax.all_to_all(outgoing, ('hst', 'dev'), split_axis=0, concat_axis=0, til...  11.1 us
    all_to_all x1, starting transfers between devices, local(): lax.all_to_all(outgoing, ('hst', 'dev'), split_axis=0, concat_axis=0, til...  6.05 us
  transfers between devices with their start and end apart: 1, of which 1 were waited for; matrix products, arithmetic and copies ran while one was open for 15% of the time, Pallas kernels for 18%

profile of v3, /device:TPU:8, one launch (start us, length us, event | category | flops | bytes accessed | tf_op | source)
XLA Modules:
  0.0 157.4 jit_solution(126388632367002551)
XLA Ops:
  1.1 1.4 copy-done.11
  2.5 4.5 %select_rows.1 = bf16[2048,768]{1,0:T(8,128)(2,1)S(1)} custom-call(s32[2048,1]{1,0:T(8,128)S(1)} %copy.22.index_ref, bf16[1024,768]{1,0:T(8,128)(2,1)S(1)} %copy-done.11), custom_call_target="tpu_custom_call" | custom-call | tf_op jit(solution)/shard_map/select_rows/pallas_call | solution.py:38
  7.0 1.7 %copy-done.1 = bf16[2048,768]{1,0:T(8,128)(2,1)} copy-done((bf16[2048,768]{1,0:T(8,128)(2,1)}, bf16[2048,768]{1,0:T(8,128)(2,1)S(1)}, u32[]{:S(2)}) %copy-start.1) | copy-done | bytes 3145752
  8.7 6.0 %all-to-all-start = ((bf16[32,64,768]{2,1,0:T(8,128)(2,1)}), bf16[32,64,768]{2,1,0:T(8,128)(2,1)S(1)}, u32[]{:S(2)}, u32[]{:S(2)}) async-start(bf16[32,64,768]{2,1,0:T(8,128)(2,1)} %bitcast.8), calls=%async_computation | async-start | bytes 6291456 | tf_op jit(solution)/shard_map/all_to_all | solution.py:332
  14.8 1.4 copy.24.place_ref
  16.2 1.3 copy.23.index_ref
  18.6 2.0 %copy.27.self_ref = bf16[1024,153]{1,0:T(8,128)(2,1)} copy(bf16[1024,153]{0,1:T(8,128)(2,1)} %param.30) | data formatting | bytes 626688 | tf_op args[14]
  20.6 2.0 %copy.28.neigh_ref = bf16[1024,153]{1,0:T(8,128)(2,1)} copy(bf16[1024,153]{0,1:T(8,128)(2,1)} %param.31) | data formatting | bytes 626688 | tf_op args[15]
  23.2 13.7 %gather_fusion = bf16[2048,768]{1,0:T(8,128)(2,1)} fusion(bf16[4096,768]{1,0:T(8,128)(2,1)} %param.16, s32[2048]{0:T(1024)S(1)} %fusion), kind=kCustom, calls=%fused_computation | custom fusion | bytes 6299648 | tf_op jit(solution)/shard_map/gather | solution.py:335
  36.9 6.0 %count_matrix.3.counts_ref = bf16[512,2304]{1,0:T(8,128)(2,1)S(1)} custom-call(s32[512,15]{1,0:T(8,128)S(1)} %copy.26.index_ref), custom_call_target="tpu_custom_call" | custom-call | flops 1769472000 | bytes 2359296 | tf_op jit(solution)/shard_map/count_matrix/pallas_call | solution.py:76
  42.9 1.4 copy-done.5
  44.3 22.4 %count_matrix.2.counts_ref = bf16[2048,2048]{1,0:T(8,128)(2,1)S(1)} custom-call(s32[2048,15]{1,0:T(8,128)S(1)} %copy-done.12), custom_call_target="tpu_custom_call" | custom-call | flops 6291456000 | bytes 8388608 | tf_op jit(solution)/shard_map/count_matrix/pallas_call | solution.py:76
  66.7 3.3 %copy-done.2 = bf16[2048,2048]{1,0:T(8,128)(2,1)} copy-done((bf16[2048,2048]{1,0:T(8,128)(2,1)}, bf16[2048,2048]{1,0:T(8,128)(2,1)S(1)}, u32[]{:S(2)}) %copy-start.2) | copy-done | bytes 8388632
  70.0 1.9 %broadcast_select_fusion.hot_ref = bf16[2048,768]{1,0:T(8,128)(2,1)} fusion(bf16[2048,768]{1,0:T(8,128)(2,1)S(1)} %copy-done.15, pred[2048]{0:T(1024)(128)(4,1)S(1)} %get-tuple-element.14), kind=kLoop, calls=%fused_computation.1 | loop fusion | flops 1572864 | bytes 6293504 | tf_op jit(solution)/shard_map/jit(_where)/select_n | solution.py:334
  71.9 11.1 %all-to-all-done = bf16[32,64,768]{2,1,0:T(8,128)(2,1)S(1)} async-done(((bf16[32,64,768]{2,1,0:T(8,128)(2,1)}), bf16[32,64,768]{2,1,0:T(8,128)(2,1)S(1)}, u32[]{:S(2)}, u32[]{:S(2)}) %all-to-all-start) | async-done | bytes 3145760 | tf_op jit(solution)/shard_map/all_to_all | solution.py:332
  83.0 1.9 %copy-done = bf16[2048,768]{1,0:T(8,128)(2,1)S(1)} copy-done((bf16[2048,768]{1,0:T(8,128)(2,1)S(1)}, bf16[2048,768]{1,0:T(8,128)(2,1)}, u32[]{:S(2)}) %copy-start) | copy-done | bytes 3145752
  84.9 1.2 copy-done.4
  86.2 1.4 copy-done.9
  87.6 1.4 copy-done.10
  89.0 29.6 %first_layer.1 = (f32[2048,1024]{1,0:T(8,128)}, f32[2,1024]{1,0:T(2,128)S(1)}) custom-call(bf16[2048,768]{1,0:T(8,128)(2,1)S(1)} %bitcast.7, s32[2048,1]{1,0:T(8,128)S(1)} %copy-done.4, bf16[2048,768]{1,0:T(8,128)(2,1)S(1)} %copy-done, bf16[2048,2048]{1,0:T(8,128)(2,1)} %copy-done.2, bf16[768,1024]{1,0:T(8,128)(2,1)S(1)} %copy-done.9, ...), custom_call_target="tpu_custom_call" | custom-call | tf_op jit(solution)/shard_map/first_layer/pallas_call | solution.py:130
  118.5 11.9 %sum_stats.1.stats_ref = f32[2,1024]{1,0:T(2,128)S(1)} custom-call(f32[2,1024]{1,0:T(2,128)S(1)} %get-tuple-element.10.own_ref), custom_call_target="tpu_custom_call" | custom-call | tf_op jit(solution)/shard_map/sum_stats/pallas_call | solution.py:185
  130.5 3.4 %copy-done.3 = f32[2048,1024]{1,0:T(8,128)S(1)} copy-done((f32[2048,1024]{1,0:T(8,128)S(1)}, f32[2048,1024]{1,0:T(8,128)}, u32[]{:S(2)}) %copy-start.3) | copy-done | bytes 8388632
  133.9 3.2 %norm_layer.1 = (bf16[2048,1024]{1,0:T(8,128)(2,1)S(1)}, bf16[256,1024]{1,0:T(8,128)(2,1)S(1)}) custom-call(f32[2048,1024]{1,0:T(8,128)S(1)} %copy-done.3, f32[2,1024]{1,0:T(2,128)S(1)} %sum_stats.1.stats_ref, f32[1,1024]{1,0:T(1,128)S(1)} %bitcast.9, f32[1,1024]{1,0:T(1,128)S(1)} %bitcast.10, s32[256,1]{1,0:T(8,128)S(1)} %copy.25.picks_ref), custom_call_target="tpu_custom_call" | custom-call | tf_op jit(solution)/shard_map/norm_layer/pallas_call | solution.py:234
  137.2 19.3 %last_layer.1 = f32[512,153]{1,0:T(8,128)S(1)} custom-call(bf16[256,1024]{1,0:T(8,128)(2,1)S(1)} %get-tuple-element.11.boundary_ref, bf16[2048,1024]{1,0:T(8,128)(2,1)S(1)} %get-tuple-element.12.hidden_ref, bf16[512,2304]{1,0:T(8,128)(2,1)S(1)} %copy-done.6, bf16[1024,153]{1,0:T(8,128)(2,1)S(1)} %copy-done.7, bf16[1024,153]{1,0:T(8,128)(2,1)S(1)} %copy-done.8), custom_call_target="tpu_custom_call" | custom-call | tf_op jit(solution)/shard_map/last_layer/pallas_call | solution.py:291
  (39 shorter events, 3.8 us)
Async XLA Ops:
  1.1 1.4 copy-start.11
  7.0 1.7 %copy-start.1 = (bf16[2048,768]{1,0:T(8,128)(2,1)}, bf16[2048,768]{1,0:T(8,128)(2,1)S(1)}, u32[]{:S(2)}) copy-start(bf16[2048,768]{1,0:T(8,128)(2,1)S(1)} %select_rows.1) | copy-start | bytes 9437188
  8.7 6.1 %copy-start.17 = (s32[2048]{0:T(1024)S(1)}, s32[2048]{0:T(1024)}, u32[]{:S(2)}) copy-start(s32[2048]{0:T(1024)} %param.21) | copy-start | bytes 24580
  8.7 6.1 %copy-start.18 = (s32[2048]{0:T(1024)S(1)}, s32[2048]{0:T(1024)}, u32[]{:S(2)}) copy-start(s32[2048]{0:T(1024)} %param.20) | copy-start | bytes 24580
  8.7 6.1 %copy-start.19 = (s32[2048]{0:T(1024)S(1)}, s32[2048]{0:T(1024)}, u32[]{:S(2)}) copy-start(s32[2048]{0:T(1024)} %param.18) | copy-start | bytes 24580
  8.7 7.5 %copy-start.16 = (s32[2048,15]{0,1:T(8,128)S(1)}, s32[2048,15]{0,1:T(8,128)}, u32[]{:S(2)}) copy-start(s32[2048,15]{0,1:T(8,128)} %param.23) | copy-start | bytes 368644
  8.7 8.8 %copy-start.20 = (s32[1,256]{1,0:T(1,128)S(1)}, s32[1,256]{1,0:T(1,128)}, u32[]{:S(2)}) copy-start(s32[1,256]{1,0:T(1,128)} %param.25) | copy-start | bytes 3076
  8.7 74.3 %all-to-all-start = ((bf16[32,64,768]{2,1,0:T(8,128)(2,1)}), bf16[32,64,768]{2,1,0:T(8,128)(2,1)S(1)}, u32[]{:S(2)}, u32[]{:S(2)}) async-start(bf16[32,64,768]{2,1,0:T(8,128)(2,1)} %bitcast.8), calls=%async_computation | async-start | bytes 6291456 | tf_op jit(solution)/shard_map/all_to_all | solution.py:332
  36.9 7.4 %copy-start.12 = (s32[2048,15]{1,0:T(8,128)S(1)}, s32[2048,15]{1,0:T(8,128)}, u32[]{:S(2)}) copy-start(s32[2048,15]{1,0:T(8,128)} %copy.23.index_ref) | copy-start | bytes 368644
  42.9 1.4 copy-start.5
  44.3 25.7 %copy-start.15 = (bf16[2048,768]{1,0:T(8,128)(2,1)S(1)}, bf16[2048,768]{1,0:T(8,128)(2,1)}, u32[]{:S(2)}) copy-start(bf16[2048,768]{1,0:T(8,128)(2,1)} %gather_fusion) | copy-start | bytes 9437188
  66.7 3.3 %copy-start.2 = (bf16[2048,2048]{1,0:T(8,128)(2,1)}, bf16[2048,2048]{1,0:T(8,128)(2,1)S(1)}, u32[]{:S(2)}) copy-start(bf16[2048,2048]{1,0:T(8,128)(2,1)S(1)} %count_matrix.2.counts_ref) | copy-start | bytes 25165828
  83.0 1.9 %copy-start = (bf16[2048,768]{1,0:T(8,128)(2,1)S(1)}, bf16[2048,768]{1,0:T(8,128)(2,1)}, u32[]{:S(2)}) copy-start(bf16[2048,768]{1,0:T(8,128)(2,1)} %broadcast_select_fusion.hot_ref) | copy-start | bytes 9437188
  84.9 1.2 copy-start.4
  86.2 1.4 copy-start.9
  87.6 1.4 copy-start.10
  89.0 41.5 %copy-start.13 = (f32[1024]{0:T(1024)S(1)}, f32[1024]{0:T(1024)}, u32[]{:S(2)}) copy-start(f32[1024]{0:T(1024)} %param.28) | copy-start | bytes 12292
  89.0 41.5 %copy-start.14 = (f32[1024]{0:T(1024)S(1)}, f32[1024]{0:T(1024)}, u32[]{:S(2)}) copy-start(f32[1024]{0:T(1024)} %param.29) | copy-start | bytes 12292
  130.5 3.4 %copy-start.3 = (f32[2048,1024]{1,0:T(8,128)S(1)}, f32[2048,1024]{1,0:T(8,128)}, u32[]{:S(2)}) copy-start(f32[2048,1024]{1,0:T(8,128)} %get-tuple-element.9.pre_ref) | copy-start | bytes 25165828
  133.9 3.3 %copy-start.6 = (bf16[512,2304]{1,0:T(8,128)(2,1)S(1)}, bf16[512,2304]{1,0:T(8,128)(2,1)}, u32[]{:S(2)}) copy-start(bf16[512,2304]{1,0:T(8,128)(2,1)} %copy-done.5) | copy-start | bytes 7077892
  133.9 3.3 %copy-start.7 = (bf16[1024,153]{1,0:T(8,128)(2,1)S(1)}, bf16[1024,153]{1,0:T(8,128)(2,1)}, u32[]{:S(2)}) copy-start(bf16[1024,153]{1,0:T(8,128)(2,1)} %copy.27.self_ref) | copy-start | bytes 940036
  133.9 3.3 %copy-start.8 = (bf16[1024,153]{1,0:T(8,128)(2,1)S(1)}, bf16[1024,153]{1,0:T(8,128)(2,1)}, u32[]{:S(2)}) copy-start(bf16[1024,153]{1,0:T(8,128)(2,1)} %copy.28.neigh_ref) | copy-start | bytes 940036
